TPU v7x, 32 devices: a whole 2x2x4 slice. The times are simulated.
32 devices in a mesh: samp: 8 (over z, x), win: 1, snp: 4 (over y, core).
Axes of the slice: x: 2, y: 2, z: 4, core: 2. Of those that a mesh axis runs over, the one named last changes fastest.
Arguments:
- dosages: bfloat16 [4096, 4096], P('samp', ('win', 'snp')), may hold values from 0 to 2
Outputs:
- r_squared: float32 [1, 4096, 4096], P('win', 'samp', 'snp')
- band_r_squared: float32 [1, 1024, 4096], P('win', 'samp', 'snp')
All inputs are finite; a program needn't handle non-finite values.
Results may differ from a plain program's by a relative error of at most 0.0003.
Values may be sent and summed in bfloat16 or wider, within the bound.
A program may use at most 128 MiB of HBM per device.

v0:
```python
import jax
import jax.numpy as jnp
from jax import lax
from jax.sharding import PartitionSpec as P

OV = 1024
var_floor = 0.05


def passed_along(shard, axis, by):
    devices = lax.axis_size(axis)
    return lax.ppermute(shard, axis, [(i, (i + by) % devices) for i in range(devices)])


def squared_corr(gram, col_sum, col_sq, row_sum, row_sq, count):
    col_mean = col_sum / count
    row_mean = row_sum / count
    col_var = jnp.maximum(col_sq / count - col_mean * col_mean, var_floor)
    row_var = jnp.maximum(row_sq / count - row_mean * row_mean, var_floor)
    covar = gram / count - col_mean[:, None] * row_mean[None, :]
    return covar * covar / (col_var[:, None] * row_var[None, :])


def column_stats(block):
    return (
        jnp.sum(block, axis=0, dtype=jnp.float32),
        jnp.sum(jnp.square(block.astype(jnp.float32)), axis=0),
    )


def pair_sums(columns, own_rows):
    return lax.dot_general(
        columns, own_rows, (((0,), (0,)), ((), ())), preferred_element_type=jnp.float32
    )


def shards(dosages):
    samples_here = dosages.shape[0]
    block_width = dosages.shape[1]
    shard_count = lax.axis_size("samp")
    count = jnp.float32(samples_here * shard_count)
    whole = lax.all_gather(dosages, "snp", axis=1, tiled=True)
    window_width = whole.shape[1]
    band = passed_along(whole[:, :OV], "win", -1)
    own_sum, own_sq = column_stats(dosages)
    total_sum, total_sq = lax.psum((own_sum, own_sq), "samp")
    win_sum, win_sq = (
        lax.all_gather(total_sum, "snp", axis=0, tiled=True),
        lax.all_gather(total_sq, "snp", axis=0, tiled=True),
    )
    next_sum, next_sq = passed_along((win_sum[:OV], win_sq[:OV]), "win", -1)
    win_cols = window_width // shard_count
    band_cols = OV // shard_count
    merged = jnp.concatenate(
        (
            whole.reshape(samples_here, shard_count, win_cols),
            band.reshape(samples_here, shard_count, band_cols),
        ),
        axis=2,
    ).reshape(samples_here, shard_count * (win_cols + band_cols))
    summed = lax.psum_scatter(pair_sums(merged, dosages), "samp", scatter_dimension=0, tiled=True)
    win_gram = summed[:win_cols]
    band_gram = summed[win_cols:]
    col_index = lax.axis_index("samp")
    row_index = lax.axis_index("snp")
    row_sum = lax.dynamic_slice_in_dim(win_sum, row_index * block_width, block_width, 0)
    row_sq = lax.dynamic_slice_in_dim(win_sq, row_index * block_width, block_width, 0)
    col_sum = lax.dynamic_slice_in_dim(win_sum, col_index * win_cols, win_cols, 0)
    col_sq = lax.dynamic_slice_in_dim(win_sq, col_index * win_cols, win_cols, 0)
    band_sum = lax.dynamic_slice_in_dim(next_sum, col_index * band_cols, band_cols, 0)
    band_sq = lax.dynamic_slice_in_dim(next_sq, col_index * band_cols, band_cols, 0)
    whole_out = squared_corr(win_gram, col_sum, col_sq, row_sum, row_sq, count)
    band_out = squared_corr(band_gram, band_sum, band_sq, row_sum, row_sq, count)
    return (whole_out[None], band_out[None])


def solution(mesh):
    return jax.shard_map(
        shards,
        mesh=mesh,
        in_specs=(P("samp", ("win", "snp")),),
        out_specs=(P("win", "samp", "snp"), P("win", "samp", "snp")),
        check_vma=False,
    )
```

profile of v0, /device:TPU:0, one launch (start us, length us, event | category | flops | bytes accessed | tf_op | source)
XLA Modules:
  0.0 419.4 jit_solution(9305339508099588703)
XLA Ops:
  7.2 0.0 all-gather.2.cloned.1.call-start
  7.2 0.7 all-gather.2.cloned.1.call-update
  7.9 0.0 reduce-scatter.2.cloned.1.call-start
  7.9 38.8 %all-gather.2.cloned.1.call-done = bf16[512,4096]{1,0:T(8,128)(2,1)} async-done(((bf16[512,1024]{1,0:T(8,128)(2,1)}), bf16[512,4096]{1,0:T(8,128)(2,1)}) %all-gather.2.cloned.1.call-update) | async-done | bytes 4194320 | tf_op jit(solution)/shard_map/all_gather | solution.py:42
  46.8 1.3 slice.20
  48.0 0.1 collective-permute-start
  48.1 4.4 %copy.3 = bf16[64,8,8,512]{3,2,1,0:T(8,128)(2,1)S(1)} copy(bf16[64,8,8,512]{3,1,2,0:T(8,128)(2,1)} %bitcast.14) | data formatting | bytes 8388608
  52.5 0.0 collective-permute-done
  52.6 0.3 copy.4
  52.8 0.5 pad_maximum_fusion
  53.3 0.0 copy-start
  53.3 1.2 copy.5
  54.5 0.0 copy-done
  54.5 9.9 %fusion.10 = f32[5120,1024]{1,0:T(8,128)} fusion(bf16[512,5120]{1,0:T(8,128)(2,1)S(1)} %bitcast.15, bf16[512,1024]{1,0:T(8,128)(2,1)S(1)} %copy-done), kind=kOutput, calls=%fused_computation.21 | convolution fusion | flops 5368709120 | bytes 27262976 | tf_op jit(solution)/shard_map/dot_general | solution.py:32
  64.4 0.0 reduce-scatter.2.cloned.1.call-update
  64.4 0.3 convert_reduce_fusion
  64.8 22.7 %all-reduce = (f32[1024]{0:T(1024)S(1)}, f32[1024]{0:T(1024)S(1)}) all-reduce(f32[1024]{0:T(1024)S(1)} %get-tuple-element.3, f32[1024]{0:T(1024)S(1)} %get-tuple-element.2), channel_id=1, replica_groups=mesh['samp'=8,'win'=1,'snp'=4] {'samp'}, use_global_device_ids=true, to_apply=%region_4.0 | all-reduce | flops 2048 | bytes 16384 | tf_op jit(solution)/shard_map/psum | solution.py:46
  87.5 5.2 %all_gather.10 = f32[4096]{0:T(1024)S(1)} all-gather(f32[1024]{0:T(1024)S(1)} %get-tuple-element.5), channel_id=1, replica_groups=mesh['samp'=8,'win'=1,'snp'=4] {'snp'}, dimensions={0}, use_global_device_ids=true | all-gather | bytes 20480 | tf_op jit(solution)/shard_map/all_gather | solution.py:48
  92.7 5.2 %all_gather.11 = f32[4096]{0:T(1024)S(1)} all-gather(f32[1024]{0:T(1024)S(1)} %get-tuple-element.4), channel_id=1, replica_groups=mesh['samp'=8,'win'=1,'snp'=4] {'snp'}, dimensions={0}, use_global_device_ids=true | all-gather | bytes 20480 | tf_op jit(solution)/shard_map/all_gather | solution.py:49
  97.9 0.0 collective-permute-start.1
  97.9 0.0 collective-permute-start.2
  97.9 0.1 dynamic-slice_multiply_fusion.1
  98.0 0.0 collective-permute-done.1
  98.0 0.0 collective-permute-done.2
  98.0 0.1 dynamic-slice_multiply_fusion.2
  98.1 308.9 %reduce-scatter.2.cloned.1.call-done = f32[640,1024]{1,0:T(8,128)} async-done(((f32[5120,1024]{1,0:T(8,128)}), f32[640,1024]{1,0:T(8,128)}) %reduce-scatter.2.cloned.1.call-update) | async-done | bytes 2621456 | tf_op jit(solution)/shard_map/reduce_scatter | solution.py:61
  407.0 3.5 fusion.4
  410.5 2.0 fusion.8
  (1 shorter events, 0.0 us)
Async XLA Ops:
  7.2 39.6 %all-gather.2.cloned.1.call-start = ((), (), s32[]{:S(2)}) async-start(), calls=%async_computation.1 | async-start | bytes 5242880 | tf_op jit(solution)/shard_map/all_gather | solution.py:42
  7.9 399.1 %reduce-scatter.2.cloned.1.call-start = ((), (), s32[]{:S(2)}) async-start(), calls=%async_computation.2 | async-start | bytes 23592960 | tf_op jit(solution)/shard_map/reduce_scatter | solution.py:61
  48.0 4.5 %collective-permute-start = (bf16[512,1024]{1,0:T(8,128)(2,1)S(1)}, bf16[512,1024]{1,0:T(8,128)(2,1)S(1)}, u32[]{:S(2)}, u32[]{:S(2)}) collective-permute-start(bf16[512,1024]{1,0:T(8,128)(2,1)S(1)} %slice.20), channel_id=1, source_target_pairs={{0,0},{1,1},{2,2},{3,3},{4,4},{5,5},{6,6},{7,7},{8,8},{9,9},{10,10... | collective-permute-start | bytes 3145736 | tf_op jit(solution)/shard_map/ppermute | solution.py:12
  53.3 1.2 copy-start
  97.9 0.1 collective-permute-start.1
  97.9 0.1 collective-permute-start.2
Sparse Core Ops, SparseCore 0:
  9.5 37.1 all-gather.1
  64.6 342.4 reduce-scatter.1
where the time goes:
time: 420 us; the launch traced here: 419 us
  waiting for transfers between devices  348 us (83%)
  blocking collectives  33.1 us (8%)
  between operations  14.1 us (3%)
  matrix products  9.9 us (2%)
  local copies, waits for them, and re-layouts  7.19 us (2%)
  other arithmetic  6.47 us (2%)
    reduce_scatter x1, waiting for transfers between devices, shards(): lax.psum_scatter(pair_sums(merged, dosages), 'samp', scatter_dimension=0,...  309 us
    all_gather x1, waiting for transfers between devices, shards(): whole = lax.all_gather(dosages, 'snp', axis=1, tiled=True)  38.8 us
    psum x1, blocking collectives, shards(): total_sum, total_sq = lax.psum((own_sum, own_sq), 'samp')  22.7 us
    dot_general x1, matrix products, pair_sums(): lax.dot_general(columns, own_rows, (((0,), (0,)), ((), ())), preferred_el...  9.9 us
  transfers between devices with their start and end apart: 5, of which 2 were waited for; matrix products, arithmetic and copies ran while one was open for 1% of the time, Pallas kernels for 0%

commit v1 on v0

--- a/solution.py
+++ b/solution.py
@@ -39,7 +39,14 @@
     block_width = dosages.shape[1]
     shard_count = lax.axis_size("samp")
     count = jnp.float32(samples_here * shard_count)
-    whole = lax.all_gather(dosages, "snp", axis=1, tiled=True)
+    count_2 = lax.axis_size("snp")
+    right = [(i_2, (i_2 + 1) % count_2) for i_2 in range(count_2)]
+    parts = [dosages]
+    for far in range(1, count_2):
+        parts = [lax.ppermute(parts[0], "snp", right), *parts]
+    full = jnp.concatenate(parts, axis=1)
+    shift = (lax.axis_index("snp") + 1) * parts[-1].shape[1]
+    whole = jnp.roll(full, shift, axis=1)
     window_width = whole.shape[1]
     band = passed_along(whole[:, :OV], "win", -1)
     own_sum, own_sq = column_stats(dosages)

time: 420 us -> 428 us (1.019)
  waiting for transfers between devices: 348 us -> 354 us
    ppermute x0 -> x3, waiting for transfers between devices: none -> 43.1 us  [shards(): parts = [lax.ppermute(parts[0], 'snp', right), *parts]]
    all_gather x1 -> x0, waiting for transfers between devices: 38.8 us -> none  [shards(): whole = lax.all_gather(dosages, 'snp', axis=1, tiled=True)]
  transfers between devices with their start and end apart: 5 -> 7, of which waited for: 2 -> 4; matrix products, arithmetic and copies ran while one was open for 1% -> 1% of each run, Pallas kernels for 0% -> 0%
where the time goes in v1:
time: 428 us
  waiting for transfers between devices  354 us (83%)
  blocking collectives  33.9 us (8%)
  between operations  14.2 us (3%)
  matrix products  9.92 us (2%)
  local copies, waits for them, and re-layouts  8.27 us (2%)
  other arithmetic  6.47 us (2%)
    reduce_scatter x1, waiting for transfers between devices, shards(): lax.psum_scatter(pair_sums(merged, dosages), 'samp', scatter_dimension=0,...  311 us
    ppermute x3, waiting for transfers between devices, shards(): parts = [lax.ppermute(parts[0], 'snp', right), *parts]  43.1 us
    psum x1, blocking collectives, shards(): total_sum, total_sq = lax.psum((own_sum, own_sq), 'samp')  23.5 us
    dot_general x1, matrix products, pair_sums(): lax.dot_general(columns, own_rows, (((0,), (0,)), ((), ())), preferred_el...  9.92 us
  transfers between devices with their start and end apart: 7, of which 4 were waited for; matrix products, arithmetic and copies ran while one was open for 1% of the time, Pallas kernels for 0%

profile of v1, /device:TPU:0, one launch (start us, length us, event | category | flops | bytes accessed | tf_op | source)
XLA Modules:
  0.0 427.7 jit_solution(14432920104413196290)
XLA Ops:
  7.2 0.0 copy-start
  7.2 0.0 reduce-scatter.2.cloned.1.call-start
  7.2 0.5 collective-permute-start
  7.8 14.6 %collective-permute-done = bf16[512,1024]{1,0:T(8,128)(2,1)S(1)} collective-permute-done((bf16[512,1024]{1,0:T(8,128)(2,1)}, bf16[512,1024]{1,0:T(8,128)(2,1)S(1)}, u32[]{:S(2)}, u32[]{:S(2)}) %collective-permute-start) | collective-permute-done | bytes 1048608 | tf_op jit(solution)/shard_map/ppermute | solution.py:46
  22.4 0.0 collective-permute-start.1
  22.4 14.2 %collective-permute-done.1 = bf16[512,1024]{1,0:T(8,128)(2,1)S(1)} collective-permute-done((bf16[512,1024]{1,0:T(8,128)(2,1)S(1)}, bf16[512,1024]{1,0:T(8,128)(2,1)S(1)}, u32[]{:S(2)}, u32[]{:S(2)}) %collective-permute-start.1) | collective-permute-done | bytes 1048608 | tf_op jit(solution)/shard_map/ppermute | solution.py:46
  36.6 0.0 collective-permute-start.2
  36.6 14.3 %collective-permute-done.2 = bf16[512,1024]{1,0:T(8,128)(2,1)} collective-permute-done((bf16[512,1024]{1,0:T(8,128)(2,1)S(1)}, bf16[512,1024]{1,0:T(8,128)(2,1)}, u32[]{:S(2)}, u32[]{:S(2)}) %collective-permute-start.2) | collective-permute-done | bytes 1048608 | tf_op jit(solution)/shard_map/ppermute | solution.py:46
  51.0 1.3 constant_dynamic-update-slice_fusion.7
  52.3 0.1 constant_dynamic-update-slice_fusion.6
  52.3 0.1 constant_dynamic-update-slice_fusion.5
  52.4 1.3 constant_dynamic-update-slice_fusion.4
  53.7 1.3 constant_dynamic-update-slice_fusion.3
  55.0 0.1 constant_dynamic-update-slice_fusion.2
  55.1 0.1 constant_dynamic-update-slice_fusion.1
  55.2 0.0 copy-done
  55.2 0.1 constant_dynamic-update-slice_fusion
  55.3 0.1 constant_dynamic-slice_fusion
  55.3 0.1 collective-permute-start.3
  55.4 0.3 constant_dynamic-slice_fusion.1
  55.7 2.2 copy.3
  57.9 0.0 collective-permute-done.3
  58.0 0.3 copy.4
  58.2 0.5 pad_maximum_fusion
  58.7 1.2 copy.5
  59.9 9.9 %fusion.10 = f32[5120,1024]{1,0:T(8,128)} fusion(bf16[512,5120]{1,0:T(8,128)(2,1)S(1)} %bitcast.15, bf16[512,1024]{1,0:T(8,128)(2,1)S(1)} %copy-done), kind=kOutput, calls=%fused_computation.31 | convolution fusion | flops 5368709120 | bytes 27262976 | tf_op jit(solution)/shard_map/dot_general | solution.py:32
  69.8 0.0 reduce-scatter.2.cloned.1.call-update
  69.8 0.3 convert_reduce_fusion
  70.1 23.5 %all-reduce = (f32[1024]{0:T(1024)S(1)}, f32[1024]{0:T(1024)S(1)}) all-reduce(f32[1024]{0:T(1024)S(1)} %get-tuple-element.3, f32[1024]{0:T(1024)S(1)} %get-tuple-element.2), channel_id=1, replica_groups=mesh['samp'=8,'win'=1,'snp'=4] {'samp'}, use_global_device_ids=true, to_apply=%region_4.5 | all-reduce | flops 2048 | bytes 16384 | tf_op jit(solution)/shard_map/psum | solution.py:53
  93.7 5.2 %all_gather.6 = f32[4096]{0:T(1024)S(1)} all-gather(f32[1024]{0:T(1024)S(1)} %get-tuple-element.5), channel_id=1, replica_groups=mesh['samp'=8,'win'=1,'snp'=4] {'snp'}, dimensions={0}, use_global_device_ids=true | all-gather | bytes 20480 | tf_op jit(solution)/shard_map/all_gather | solution.py:55
  98.9 5.2 %all_gather.7 = f32[4096]{0:T(1024)S(1)} all-gather(f32[1024]{0:T(1024)S(1)} %get-tuple-element.4), channel_id=1, replica_groups=mesh['samp'=8,'win'=1,'snp'=4] {'snp'}, dimensions={0}, use_global_device_ids=true | all-gather | bytes 20480 | tf_op jit(solution)/shard_map/all_gather | solution.py:56
  104.1 0.0 collective-permute-start.4
  104.1 0.0 collective-permute-start.5
  104.1 0.1 dynamic-slice_multiply_fusion.1
  104.2 0.0 collective-permute-done.4
  104.2 0.0 collective-permute-done.5
  104.2 0.1 dynamic-slice_multiply_fusion.2
  104.3 311.0 %reduce-scatter.2.cloned.1.call-done = f32[640,1024]{1,0:T(8,128)} async-done(((f32[5120,1024]{1,0:T(8,128)}), f32[640,1024]{1,0:T(8,128)}) %reduce-scatter.2.cloned.1.call-update) | async-done | bytes 2621456 | tf_op jit(solution)/shard_map/reduce_scatter | solution.py:68
  415.3 3.5 fusion.4
  418.8 2.0 fusion.8
  (1 shorter events, 0.0 us)
Async XLA Ops:
  7.2 48.0 %copy-start = (bf16[512,1024]{1,0:T(8,128)(2,1)S(1)}, bf16[512,1024]{1,0:T(8,128)(2,1)}, u32[]{:S(2)}) copy-start(bf16[512,1024]{1,0:T(8,128)(2,1)} %param.1) | copy-start | bytes 3145732
  7.2 408.1 %reduce-scatter.2.cloned.1.call-start = ((), (), s32[]{:S(2)}) async-start(), calls=%async_computation.1 | async-start | bytes 23592960 | tf_op jit(solution)/shard_map/reduce_scatter | solution.py:68
  7.2 15.2 %collective-permute-start = (bf16[512,1024]{1,0:T(8,128)(2,1)}, bf16[512,1024]{1,0:T(8,128)(2,1)S(1)}, u32[]{:S(2)}, u32[]{:S(2)}) collective-permute-start(bf16[512,1024]{1,0:T(8,128)(2,1)} %param.1), channel_id=1, source_target_pairs={{0,1},{1,2},{2,3},{3,0},{4,5},{5,6},{6,7},{7,4},{8,9},{9,10},{10,1... | collective-permute-start | bytes 3145736 | tf_op jit(solution)/shard_map/ppermute | solution.py:46
  22.4 14.2 %collective-permute-start.1 = (bf16[512,1024]{1,0:T(8,128)(2,1)S(1)}, bf16[512,1024]{1,0:T(8,128)(2,1)S(1)}, u32[]{:S(2)}, u32[]{:S(2)}) collective-permute-start(bf16[512,1024]{1,0:T(8,128)(2,1)S(1)} %collective-permute-done), channel_id=1, source_target_pairs={{0,1},{1,2},{2,3},{3,0},{4,5},{5,6},{6,7},{7,4},{8,9},{9,10},{10,1... | collective-permute-start | bytes 3145736 | tf_op jit(solution)/shard_map/ppermute | solution.py:46
  36.6 14.3 %collective-permute-start.2 = (bf16[512,1024]{1,0:T(8,128)(2,1)S(1)}, bf16[512,1024]{1,0:T(8,128)(2,1)}, u32[]{:S(2)}, u32[]{:S(2)}) collective-permute-start(bf16[512,1024]{1,0:T(8,128)(2,1)S(1)} %collective-permute-done.1), channel_id=1, source_target_pairs={{0,1},{1,2},{2,3},{3,0},{4,5},{5,6},{6,7},{7,4},{8,9},{9,10},{10,1... | collective-permute-start | bytes 3145736 | tf_op jit(solution)/shard_map/ppermute | solution.py:46
  55.3 2.6 collective-permute-start.3
  104.1 0.1 collective-permute-start.4
  104.1 0.1 collective-permute-start.5
Sparse Core Ops, SparseCore 0:
  69.9 345.3 reduce-scatter.1
